TPU v7x, 32 devices: a whole 2x2x4 slice. The times are simulated.
32 devices in a mesh: groups: 2 (over x), seq: 16 (over z, y, core).
Axes of the slice: x: 2, y: 2, z: 4, core: 2. Of those that a mesh axis runs over, the one named last changes fastest.
Arguments:
- queries: bfloat16 [64, 128, 576], P('groups', 'seq'), parts along dimension 0, may hold values from -8 to 8
- prefix_pool: bfloat16 [1024, 64, 576], P(('groups', 'seq')), parts along dimension 0, may hold values from -6 to 6
- block_table: int32 [8, 128], P('groups'), parts along dimension 0, may hold values from 0 to 511, as said below
- prefix_of: int32 [64], P('groups'), parts along dimension 0, may hold values from 0 to 3
- suffix_cache: bfloat16 [64, 2048, 576], P('groups', 'seq'), parts along dimension 0, may hold values from -24 to 24
- suffix_len: int32 [64], P('groups'), parts along dimension 0, may hold values from 2 to 2048
Outputs:
- context: bfloat16 [64, 128, 512], P('groups', 'seq'), parts along dimension 0
There are 2 independent parts, one for each index of `groups`. A program takes and returns all parts, laid end to end along the dimension named above; each array names one. Nothing has to cross between parts.
Inputs may be any that keep to these rules, and one draw needn't show every extreme that they name: `block_table`: each of the 512 pool blocks is named exactly once in the table, and of each aligned run of 32 pool blocks exactly 8 belong to each prefix.
All inputs are finite; a program needn't handle non-finite values.
Results may differ from a plain program's by a relative error of at most 0.0033.
Values may be sent and summed in bfloat16 or wider, within the bound.
A program may use at most 128 MiB of HBM per device.

v0:
```python
import jax
import jax.numpy as jnp
from jax import lax
from jax.sharding import PartitionSpec as P

LAT = 512
score_scale = 192.0 ** (-0.5)


def body(queries, prefix_pool, block_table, prefix_of, suffix_cache, suffix_len):
    blocks_here, block_rows, channels = prefix_pool.shape
    prefix_total = block_table.shape[0]
    slots_here = suffix_cache.shape[1]
    position = lax.axis_index("seq")
    block_ids = position * blocks_here + lax.iota(jnp.int32, blocks_here)
    owners = jnp.any(block_table[:, :, None] == block_ids[None, None, :], axis=1)
    prefix_ids = lax.iota(jnp.int32, prefix_total)
    labels = jnp.sum(owners.astype(jnp.int32) * prefix_ids[:, None], axis=0)
    order = jnp.argsort(labels, stable=True)
    segment_rows = blocks_here // prefix_total * block_rows
    segments = prefix_pool[order].reshape(prefix_total, segment_rows, channels)
    request_keys = jnp.concatenate([segments[prefix_of], suffix_cache], axis=1)
    slot_ids = position * slots_here + lax.iota(jnp.int32, slots_here)
    live_slots = slot_ids[None, :] < suffix_len[:, None]
    visible = jnp.concatenate(
        [jnp.ones((live_slots.shape[0], segment_rows), bool), live_slots], axis=1
    )
    scores = (
        jnp.einsum(
            "rhw,rkw->rhk",
            lax.all_gather(queries, "seq", axis=1, tiled=True),
            request_keys,
            preferred_element_type=jnp.float32,
        )
        * score_scale
    )
    scores = jnp.where(visible[:, None, :], scores, -jnp.inf)
    highest = lax.pmax(jnp.max(scores, axis=2), "seq")
    weights = jnp.exp(scores - highest[:, :, None])
    weight_sum = jnp.sum(weights, axis=2)
    rounded = weights.astype(jnp.bfloat16)
    weighted = jnp.einsum(
        "rhk,rkl->rhl", rounded, request_keys[:, :, :LAT], preferred_element_type=jnp.float32
    )
    weight_sum, weighted = (
        lax.psum_scatter(weight_sum, "seq", scatter_dimension=1, tiled=True),
        lax.psum_scatter(weighted, "seq", scatter_dimension=1, tiled=True),
    )
    return (weighted / weight_sum[:, :, None]).astype(jnp.bfloat16)


def solution(mesh):
    return jax.shard_map(
        body,
        mesh=mesh,
        in_specs=(
            P("groups", "seq", None),
            P(("groups", "seq"), None, None),
            P("groups", None),
            P("groups"),
            P("groups", "seq", None),
            P("groups"),
        ),
        out_specs=P("groups", "seq", None),
        check_vma=False,
    )
```

profile of v0, /device:TPU:0, one launch (start us, length us, event | category | flops | bytes accessed | tf_op | source)
XLA Modules:
  0.0 271.6 jit_solution(3408118859675830077)
XLA Ops:
  6.5 0.0 copy-start
  6.5 0.0 all-gather.2.cloned.1.call-start
  6.5 0.7 all-gather.2.cloned.1.call-update
  7.3 0.0 reduce-scatter.3.cloned.1.call-start
  7.3 0.9 compare_reduce_fusion
  8.2 1.6 sort.17
  9.9 0.7 compare_select_fusion
  10.5 0.0 copy-done
  10.5 2.4 gather_fusion
  12.9 2.9 %copy.17 = bf16[4,512,576]{1,2,0:T(8,128)(2,1)S(1)} copy(bf16[4,512,576]{2,1,0:T(8,128)(2,1)} %bitcast.16) | data formatting | bytes 4718592 | tf_op jit(solution)/shard_map/reshape | solution.py:21
  15.8 0.0 copy-start.2
  15.9 8.0 %gather_fusion.1 = bf16[32,512,576]{1,2,0:T(8,128)(2,1)} fusion(bf16[4,512,576]{1,2,0:T(8,128)(2,1)S(1)} %copy.17, s32[1024]{0:T(1024)S(1)} %get-tuple-element.9), kind=kCustom, calls=%fused_computation.1 | custom fusion | bytes 37748864 | tf_op jit(solution)/shard_map/gather | solution.py:22
  23.8 0.0 copy-done.2
  23.8 0.1 broadcast_compare_fusion
  23.9 16.9 %constant_dynamic-update-slice_fusion.1 = bf16[32,640,576]{1,2,0:T(8,128)(2,1)} fusion(bf16[32,512,576]{1,2,0:T(8,128)(2,1)} %gather_fusion.1), kind=kLoop, calls=%fused_computation.20 | loop fusion | bytes 37748736
  40.8 5.0 %constant_dynamic-update-slice_fusion = bf16[32,640,576]{1,2,0:T(8,128)(2,1)} fusion(bf16[32,640,576]{1,2,0:T(8,128)(2,1)} %constant_dynamic-update-slice_fusion.1, bf16[32,128,576]{1,2,0:T(8,128)(2,1)} %param.10), kind=kLoop, calls=%fused_computation.19 | loop fusion | bytes 9437184 | tf_op jit(solution)/shard_map/concatenate | solution.py:22
  45.8 22.8 %all-gather.2.cloned.1.call-done = bf16[32,128,576]{2,1,0:T(8,128)(2,1)} async-done(((bf16[32,8,576]{2,1,0:T(8,128)(2,1)}), bf16[32,128,576]{2,1,0:T(8,128)(2,1)}) %all-gather.2.cloned.1.call-update) | async-done | bytes 4718608 | tf_op jit(solution)/shard_map/all_gather | solution.py:31
  68.5 17.1 %bitcast_reduce_fusion = (f32[32,128]{1,0:T(8,128)S(1)}, f32[32,640,128]{2,1,0:T(8,128)}) fusion(pred[32,640]{1,0:T(8,128)(4,1)S(1)} %concatenate.6, bf16[32,640,576]{1,2,0:T(8,128)(2,1)} %constant_dynamic-update-slice_fusion, bf16[32,128,576]{2,1,0:T(8,128)(2,1)} %all-gather.2.cloned.1.call-done), kind=kOutput, calls=%fused_computation.5 | convolution fusion | flops 3027759104 | bytes 38834176 | tf_op jit(solution)/shard_map/rhw,rkw->rhk/dot_general | solution.py:29
  85.6 59.2 %pmax.7 = f32[32,128]{1,0:T(8,128)S(1)} all-reduce(f32[32,128]{1,0:T(8,128)S(1)} %get-tuple-element.7), channel_id=1, replica_groups=mesh['groups'=2,'seq'=16] {'seq'}, use_global_device_ids=true, to_apply=%region_4.5 | all-reduce | flops 4096 | bytes 32768 | tf_op jit(solution)/shard_map/pmax | solution.py:38
  144.8 0.0 copy-start.3
  144.8 0.0 copy-start.1
  144.8 16.3 %fusion = f32[32,128,512]{2,1,0:T(8,128)} fusion(bf16[32,640,576]{1,2,0:T(8,128)(2,1)} %constant_dynamic-update-slice_fusion, f32[32,640,128]{2,1,0:T(8,128)} %get-tuple-element.8, f32[32,128]{1,0:T(8,128)S(1)} %pmax.7, pred[32,640]{1,0:T(8,128)(4,1)S(1)} %concatenate.6), kind=kOutput, calls=%fused_computation.2 | convolution fusion | flops 2694840320 | bytes 39882752 | tf_op jit(solution)/shard_map/rhk,rkl->rhl/dot_general | solution.py:42
  161.1 0.0 reduce-scatter.3.cloned.1.call-update
  161.1 0.0 copy-done.3
  161.1 0.6 dynamic-slice
  162.3 9.0 %fusion.3 = f32[32,128]{1,0:T(8,128)S(1)} fusion(f32[32,640,128]{2,1,0:T(8,128)} %get-tuple-element.8, f32[32,128]{1,0:T(8,128)S(1)} %pmax.7, pred[32,640]{1,0:T(8,128)(4,1)S(1)} %concatenate.6), kind=kLoop, calls=%fused_computation.8 | loop fusion | flops 10481664 | bytes 10539008 | tf_op jit(solution)/shard_map/reduce_sum | solution.py:40
  171.4 60.6 %all-reduce.1 = f32[32,128]{1,0:T(8,128)S(1)} all-reduce(f32[32,128]{1,0:T(8,128)S(1)} %fusion.3), channel_id=3, replica_groups=mesh['groups'=2,'seq'=16] {'seq'}, use_global_device_ids=true, to_apply=%region_7.8.clone | all-reduce | flops 4096 | bytes 32768
  231.9 0.1 constant_dynamic-slice_fusion
  232.0 30.9 %reduce-scatter.3.cloned.1.call-done = f32[32,8,512]{2,1,0:T(8,128)} async-done(((f32[32,128,512]{2,1,0:T(8,128)}), f32[32,8,512]{2,1,0:T(8,128)}) %reduce-scatter.3.cloned.1.call-update) | async-done | bytes 524304 | tf_op jit(solution)/shard_map/reduce_scatter | solution.py:47
  262.9 1.9 divide_convert_fusion
  264.8 0.0 copy-done.1
  (7 shorter events, 0.1 us)
Async XLA Ops:
  6.5 4.0 %copy-start = (bf16[32,64,576]{2,1,0:T(8,128)(2,1)S(1)}, bf16[32,64,576]{2,1,0:T(8,128)(2,1)}, u32[]{:S(2)}) copy-start(bf16[32,64,576]{2,1,0:T(8,128)(2,1)} %param.7) | copy-start | bytes 7077892
  6.5 62.0 %all-gather.2.cloned.1.call-start = ((), (), s32[]{:S(2)}) async-start(), calls=%async_computation.1 | async-start | bytes 5570560 | tf_op jit(solution)/shard_map/all_gather | solution.py:31
  7.3 255.7 %reduce-scatter.3.cloned.1.call-start = ((), (), s32[]{:S(2)}) async-start(), calls=%async_computation.2 | async-start | bytes 8912896 | tf_op jit(solution)/shard_map/reduce_scatter | solution.py:47
  15.8 8.0 %copy-start.2 = (s32[32]{0:T(128)S(1)}, s32[32]{0:T(128)}, u32[]{:S(2)}) copy-start(s32[32]{0:T(128)} %param.11) | copy-start | bytes 388
  144.8 16.3 %copy-start.3 = (u32[32]{0:T(128)S(1)}, u32[32]{0:T(128)}, u32[]{:S(2)}) copy-start(u32[32]{0:T(128)} %constant.30) | copy-start | bytes 388
  144.8 120.0 %copy-start.1 = (bf16[32,64,576]{2,1,0:T(8,128)(2,1)S(1)}, bf16[32,64,576]{2,1,0:T(8,128)(2,1)}, u32[]{:S(2)}) copy-start(bf16[32,64,576]{2,1,0:T(8,128)(2,1)} %param.7) | copy-start | bytes 7077892
Sparse Core Ops, SparseCore 0:
  9.5 58.9 all-gather.1
  161.2 101.6 reduce-scatter.2
where the time goes:
time: 272 us
  blocking collectives  120 us (44%)
  waiting for transfers between devices  54.4 us (20%)
  local copies, waits for them, and re-layouts  35.8 us (13%)
  matrix products  33.4 us (12%)
  other arithmetic  14.1 us (5%)
  between operations  14.1 us (5%)
    unnamed x1, blocking collectives  60.6 us
    pmax x1, blocking collectives, body(): highest = lax.pmax(jnp.max(scores, axis=2), 'seq')  59.2 us
    reduce_scatter x1, waiting for transfers between devices, body(): lax.psum_scatter(weighted, 'seq', scatter_dimension=1, tiled=True)  30.9 us
    all_gather x1, waiting for transfers between devices, body(): lax.all_gather(queries, 'seq', axis=1, tiled=True)  22.8 us
    unnamed x11, local copies, waits for them, and re-layouts  17.6 us
    dot_general x1, matrix products, body(): jnp.einsum('rhw,rkw->rhk', lax.all_gather(queries, 'seq', axis=1, tiled=T...  17.1 us
    dot_general x1, matrix products, body(): jnp.einsum('rhk,rkl->rhl', rounded, request_keys[:, :, :LAT], preferred_e...  16.3 us
    reduce_sum x1, other arithmetic, body(): weight_sum = jnp.sum(weights, axis=2)  9.02 us
  transfers between devices with their start and end apart: 2, of which 2 were waited for; matrix products, arithmetic and copies ran while one was open for 18% of the time, Pallas kernels for 0%

commit v1 on v0

--- a/solution.py
+++ b/solution.py
@@ -5,6 +5,13 @@
 
 LAT = 512
 score_scale = 192.0 ** (-0.5)
+
+
+def shifts_all_open(local_array, at_axis):
+    back = list(local_array.shape[1:])
+    back[at_axis] *= local_array.shape[0]
+    a_next = jnp.moveaxis(local_array, 0, at_axis).reshape(back)
+    return a_next
 
 
 def body(queries, prefix_pool, block_table, prefix_of, suffix_cache, suffix_len):
@@ -25,12 +32,44 @@
     visible = jnp.concatenate(
         [jnp.ones((live_slots.shape[0], segment_rows), bool), live_slots], axis=1
     )
+
+    def sources_all_build(inputs, net_axis, d0, payload, dim_at):
+        y2 = lax.axis_size(net_axis)
+        w_next, parts_out, b_now = (y2, lax.axis_index(net_axis), inputs.shape[d0])
+        local_out = range(w_next)
+        opened = map(lambda it: (it, (it + 1) % w_next), local_out)
+        arrivals = list(map(lambda it: (it, (it - 1) % w_next), range(w_next)))
+        crops = list(opened)
+        current_value = w_next // 2
+        met_up = {}
+        now = x_now = inputs
+        rr = 0
+        while rr < current_value + 1:
+            z1 = lax.ppermute(now, axis_name=net_axis, perm=crops) if rr < current_value else None
+            high = (
+                lax.ppermute(x_now, perm=arrivals, axis_name=net_axis)
+                if rr < w_next - current_value - 1
+                else None
+            )
+            met_up[-rr] = payload(now, (parts_out - rr) % w_next * b_now)
+            if 0 < rr < w_next - current_value:
+                met_up[rr] = payload(x_now, (parts_out + rr) % w_next * b_now)
+            now, x_now = (z1, high)
+            rr = rr + 1
+        met_up = jnp.stack(list(map(lambda dev: met_up[dev], sorted(met_up))), 0)
+        met_up = met_up[(jnp.arange(w_next) - parts_out + current_value) % w_next]
+        current_arr = shifts_all_open(met_up, dim_at)
+        return current_arr
+
     scores = (
-        jnp.einsum(
-            "rhw,rkw->rhk",
-            lax.all_gather(queries, "seq", axis=1, tiled=True),
-            request_keys,
-            preferred_element_type=jnp.float32,
+        sources_all_build(
+            queries,
+            "seq",
+            d0=1,
+            payload=lambda shard, start: jnp.einsum(
+                "rhw,rkw->rhk", shard, request_keys, preferred_element_type=jnp.float32
+            ),
+            dim_at=1,
         )
         * score_scale
     )

time: 272 us -> 470 us (1.73)
  matrix products: 33.4 us -> 181 us
  starting transfers between devices: 0.04 us -> 32 us
  local copies, waits for them, and re-layouts: 35.8 us -> 46 us
  other arithmetic: 14.1 us -> 21.3 us
    dot_general x1 -> x16, matrix products: 17.1 us -> 164 us  [body(): jnp.einsum('rhw,rkw->rhk', shard, request_keys, preferred_element_type=jn...]
    ppermute x0 -> x15, starting transfers between devices: none -> 32 us  [the longest x7 31.4 us: sources_all_build(): lax.ppermute(x_now, perm=arrivals, axis_name=net_axis)]
    ppermute x0 -> x15, waiting for transfers between devices: none -> 26.6 us  [the longest x8 22.7 us: sources_all_build(): lax.ppermute(now, axis_name=net_axis, perm=crops)]
    all_gather x1 -> x0, waiting for transfers between devices: 22.8 us -> none  [body(): lax.all_gather(queries, 'seq', axis=1, tiled=True)]
    gather x0 -> x1, local copies, waits for them, and re-layouts: none -> 9.19 us  [sources_all_build(): met_up = met_up[(jnp.arange(w_next) - parts_out + current_value) % w_next]]
    reduce_max x0 -> x1, other arithmetic: none -> 5.78 us  [body(): highest = lax.pmax(jnp.max(scores, axis=2), 'seq')]
    unnamed x11 -> x23, local copies, waits for them, and re-layouts: 17.6 us -> 17.5 us
  transfers between devices with their start and end apart: 2 -> 16, of which waited for: 2 -> 6; matrix products, arithmetic and copies ran while one was open for 18% -> 44% of each run, Pallas kernels for 0% -> 0%
where the time goes in v1:
time: 470 us; the launch traced here: 469 us
  matrix products  181 us (39%)
  blocking collectives  118 us (25%)
  waiting for transfers between devices  56.5 us (12%)
  local copies, waits for them, and re-layouts  46 us (10%)
  starting transfers between devices  32 us (7%)
  other arithmetic  21.3 us (5%)
  between operations  14.3 us (3%)
    dot_general x16, matrix products, body(): jnp.einsum('rhw,rkw->rhk', shard, request_keys, preferred_element_type=jn...  164 us
    unnamed x1, blocking collectives  60.5 us
    pmax x1, blocking collectives, body(): highest = lax.pmax(jnp.max(scores, axis=2), 'seq')  57.7 us
    ppermute x7, starting transfers between devices, sources_all_build(): lax.ppermute(x_now, perm=arrivals, axis_name=net_axis)  31.4 us
    reduce_scatter x1, waiting for transfers between devices, body(): lax.psum_scatter(weighted, 'seq', scatter_dimension=1, tiled=True)  29.9 us
    ppermute x8, waiting for transfers between devices, sources_all_build(): lax.ppermute(now, axis_name=net_axis, perm=crops)  22.7 us
    unnamed x23, local copies, waits for them, and re-layouts  17.5 us
    dot_general x1, matrix products, body(): jnp.einsum('rhk,rkl->rhl', rounded, request_keys[:, :, :LAT], preferred_e...  16.7 us
  transfers between devices with their start and end apart: 16, of which 6 were waited for; matrix products, arithmetic and copies ran while one was open for 44% of the time, Pallas kernels for 0%

profile of v1, /device:TPU:0, one launch (start us, length us, event | category | flops | bytes accessed | tf_op | source)
XLA Modules:
  0.0 469.2 jit_solution(13442594169713378230)
XLA Ops:
  6.5 0.5 collective-permute-start
  7.0 9.9 %collective-permute-done = bf16[32,8,576]{2,1,0:T(8,128)(2,1)S(1)} collective-permute-done((bf16[32,8,576]{2,1,0:T(8,128)(2,1)}, bf16[32,8,576]{2,1,0:T(8,128)(2,1)S(1)}, u32[]{:S(2)}, u32[]{:S(2)}) %collective-permute-start) | collective-permute-done | bytes 294944 | tf_op jit(solution)/shard_map/ppermute | solution.py:48
  17.0 4.4 collective-permute-start.8
  21.4 5.0 %collective-permute-done.1 = bf16[32,8,576]{2,1,0:T(8,128)(2,1)} collective-permute-done((bf16[32,8,576]{2,1,0:T(8,128)(2,1)S(1)}, bf16[32,8,576]{2,1,0:T(8,128)(2,1)}, u32[]{:S(2)}, u32[]{:S(2)}) %collective-permute-start.1) | collective-permute-done | bytes 294944 | tf_op jit(solution)/shard_map/ppermute | solution.py:48
  26.4 0.9 compare_reduce_fusion
  27.3 4.5 collective-permute-start.9
  31.8 4.2 collective-permute-done.2
  36.0 1.6 sort.17
  37.6 4.4 collective-permute-start.10
  42.1 3.5 collective-permute-done.3
  45.6 0.7 compare_select_fusion.1
  46.3 2.4 gather_fusion
  48.7 2.9 copy.27
  51.6 8.0 %gather_fusion.1 = bf16[32,512,576]{1,2,0:T(8,128)(2,1)} fusion(bf16[4,512,576]{1,2,0:T(8,128)(2,1)S(1)} %copy.27, s32[1024]{0:T(1024)S(1)} %get-tuple-element.7), kind=kCustom, calls=%fused_computation.1 | custom fusion | bytes 37748864 | tf_op jit(solution)/shard_map/gather | solution.py:29
  59.6 4.4 collective-permute-start.11
  64.0 16.9 %constant_dynamic-update-slice_fusion.1 = bf16[32,640,576]{1,2,0:T(8,128)(2,1)} fusion(bf16[32,512,576]{1,2,0:T(8,128)(2,1)} %gather_fusion.1), kind=kLoop, calls=%fused_computation.52 | loop fusion | bytes 37748736
  80.9 4.5 collective-permute-start.12
  85.5 0.6 concatenate.6
  86.1 3.9 collective-permute-done.12
  90.0 4.7 %collective-permute-start.13 = (bf16[32,8,576]{2,1,0:T(8,128)(2,1)S(1)}, bf16[32,8,576]{2,1,0:T(8,128)(2,1)}, u32[]{:S(2)}, u32[]{:S(2)}) collective-permute-start(bf16[32,8,576]{2,1,0:T(8,128)(2,1)S(1)} %collective-permute-done.12), channel_id=1, source_target_pairs={{0,15},{1,0},{2,1},{3,2},{4,3},{5,4},{6,5},{7,6},{8,7},{9,8},{10,9... | collective-permute-start | bytes 884744 | tf_op jit(solution)/shard_map/ppermute | solution.py:50
  94.7 0.6 pad_clamp_fusion
  95.3 5.0 %constant_dynamic-update-slice_fusion = bf16[32,640,576]{1,2,0:T(8,128)(2,1)} fusion(bf16[32,640,576]{1,2,0:T(8,128)(2,1)} %constant_dynamic-update-slice_fusion.1, bf16[32,128,576]{1,2,0:T(8,128)(2,1)} %param.10), kind=kLoop, calls=%fused_computation.51 | loop fusion | bytes 9437184 | tf_op jit(solution)/shard_map/concatenate | solution.py:29
  100.3 4.4 collective-permute-start.14
  104.7 10.2 %fusion.26 = f32[16,32,8,640]{3,2,1,0:T(8,128)} fusion(bf16[32,640,576]{1,2,0:T(8,128)(2,1)} %constant_dynamic-update-slice_fusion, bf16[32,8,576]{2,1,0:T(8,128)(2,1)S(1)} %collective-permute-done.7), kind=kOutput, calls=%fused_computation.48 | convolution fusion | flops 188743680 | bytes 24543232 | tf_op jit(solution)/shard_map/rhw,rkw->rhk/dot_general | solution.py:69
  115.0 10.2 %fusion.25 = f32[16,32,8,640]{3,2,1,0:T(8,128)} fusion(f32[16,32,8,640]{3,2,1,0:T(8,128)} %fusion.26, bf16[32,640,576]{1,2,0:T(8,128)(2,1)} %constant_dynamic-update-slice_fusion, bf16[32,8,576]{2,1,0:T(8,128)(2,1)S(1)} %collective-permute-done.6), kind=kOutput, calls=%fused_computation.46 | convolution fusion | flops 188743680 | bytes 24543232 | tf_op jit(solution)/shard_map/rhw,rkw->rhk/dot_general | solution.py:69
  125.2 10.3 %fusion.24 = f32[16,32,8,640]{3,2,1,0:T(8,128)} fusion(f32[16,32,8,640]{3,2,1,0:T(8,128)} %fusion.25, bf16[32,640,576]{1,2,0:T(8,128)(2,1)} %constant_dynamic-update-slice_fusion, bf16[32,8,576]{2,1,0:T(8,128)(2,1)S(1)} %collective-permute-done.5), kind=kOutput, calls=%fused_computation.44 | convolution fusion | flops 188743680 | bytes 24543232 | tf_op jit(solution)/shard_map/rhw,rkw->rhk/dot_general | solution.py:69
  135.5 10.3 %fusion.23 = f32[16,32,8,640]{3,2,1,0:T(8,128)} fusion(f32[16,32,8,640]{3,2,1,0:T(8,128)} %fusion.24, bf16[32,640,576]{1,2,0:T(8,128)(2,1)} %constant_dynamic-update-slice_fusion, bf16[32,8,576]{2,1,0:T(8,128)(2,1)} %collective-permute-done.4), kind=kOutput, calls=%fused_computation.42 | convolution fusion | flops 188743680 | bytes 24576000 | tf_op jit(solution)/shard_map/rhw,rkw->rhk/dot_general | solution.py:69
  145.7 10.3 %fusion.22 = f32[16,32,8,640]{3,2,1,0:T(8,128)} fusion(f32[16,32,8,640]{3,2,1,0:T(8,128)} %fusion.23, bf16[32,640,576]{1,2,0:T(8,128)(2,1)} %constant_dynamic-update-slice_fusion, bf16[32,8,576]{2,1,0:T(8,128)(2,1)} %collective-permute-done.3), kind=kOutput, calls=%fused_computation.40 | convolution fusion | flops 188743680 | bytes 24576000 | tf_op jit(solution)/shard_map/rhw,rkw->rhk/dot_general | solution.py:69
  156.0 10.3 %fusion.21 = f32[16,32,8,640]{3,2,1,0:T(8,128)} fusion(f32[16,32,8,640]{3,2,1,0:T(8,128)} %fusion.22, bf16[32,640,576]{1,2,0:T(8,128)(2,1)} %constant_dynamic-update-slice_fusion, bf16[32,8,576]{2,1,0:T(8,128)(2,1)} %collective-permute-done.2), kind=kOutput, calls=%fused_computation.38 | convolution fusion | flops 188743680 | bytes 24576000 | tf_op jit(solution)/shard_map/rhw,rkw->rhk/dot_general | solution.py:69
  166.3 10.3 %fusion.20 = f32[16,32,8,640]{3,2,1,0:T(8,128)} fusion(f32[16,32,8,640]{3,2,1,0:T(8,128)} %fusion.21, bf16[32,640,576]{1,2,0:T(8,128)(2,1)} %constant_dynamic-update-slice_fusion, bf16[32,8,576]{2,1,0:T(8,128)(2,1)} %collective-permute-done.1), kind=kOutput, calls=%fused_computation.36 | convolution fusion | flops 188743680 | bytes 24576000 | tf_op jit(solution)/shard_map/rhw,rkw->rhk/dot_general | solution.py:69
  176.6 10.3 %fusion.19 = f32[16,32,8,640]{3,2,1,0:T(8,128)} fusion(f32[16,32,8,640]{3,2,1,0:T(8,128)} %fusion.20, bf16[32,640,576]{1,2,0:T(8,128)(2,1)} %constant_dynamic-update-slice_fusion, bf16[32,8,576]{2,1,0:T(8,128)(2,1)S(1)} %collective-permute-done), kind=kOutput, calls=%fused_computation.34 | convolution fusion | flops 188743680 | bytes 24543232 | tf_op jit(solution)/shard_map/rhw,rkw->rhk/dot_general | solution.py:69
  186.8 10.2 %fusion.18 = f32[16,32,8,640]{3,2,1,0:T(8,128)} fusion(f32[16,32,8,640]{3,2,1,0:T(8,128)} %fusion.19, bf16[32,640,576]{1,2,0:T(8,128)(2,1)} %constant_dynamic-update-slice_fusion, bf16[32,8,576]{2,1,0:T(8,128)(2,1)S(1)} %copy-done.2), kind=kOutput, calls=%fused_computation.32 | convolution fusion | flops 188743680 | bytes 24543232 | tf_op jit(solution)/shard_map/rhw,rkw->rhk/dot_general | solution.py:69
  197.0 10.2 %fusion.17 = f32[16,32,8,640]{3,2,1,0:T(8,128)} fusion(f32[16,32,8,640]{3,2,1,0:T(8,128)} %fusion.18, bf16[32,640,576]{1,2,0:T(8,128)(2,1)} %constant_dynamic-update-slice_fusion, bf16[32,8,576]{2,1,0:T(8,128)(2,1)S(1)} %collective-permute-done.8), kind=kOutput, calls=%fused_computation.30 | convolution fusion | flops 188743680 | bytes 24543232 | tf_op jit(solution)/shard_map/rhw,rkw->rhk/dot_general | solution.py:69
  207.3 10.3 %fusion.16 = f32[16,32,8,640]{3,2,1,0:T(8,128)} fusion(f32[16,32,8,640]{3,2,1,0:T(8,128)} %fusion.17, bf16[32,640,576]{1,2,0:T(8,128)(2,1)} %constant_dynamic-update-slice_fusion, bf16[32,8,576]{2,1,0:T(8,128)(2,1)} %collective-permute-done.9), kind=kOutput, calls=%fused_computation.28 | convolution fusion | flops 188743680 | bytes 24576000 | tf_op jit(solution)/shard_map/rhw,rkw->rhk/dot_general | solution.py:69
  217.6 10.3 %fusion.15 = f32[16,32,8,640]{3,2,1,0:T(8,128)} fusion(f32[16,32,8,640]{3,2,1,0:T(8,128)} %fusion.16, bf16[32,640,576]{1,2,0:T(8,128)(2,1)} %constant_dynamic-update-slice_fusion, bf16[32,8,576]{2,1,0:T(8,128)(2,1)} %collective-permute-done.10), kind=kOutput, calls=%fused_computation.26 | convolution fusion | flops 188743680 | bytes 24576000 | tf_op jit(solution)/shard_map/rhw,rkw->rhk/dot_general | solution.py:69
  227.9 10.3 %fusion.14 = f32[16,32,8,640]{3,2,1,0:T(8,128)} fusion(f32[16,32,8,640]{3,2,1,0:T(8,128)} %fusion.15, bf16[32,640,576]{1,2,0:T(8,128)(2,1)} %constant_dynamic-update-slice_fusion, bf16[32,8,576]{2,1,0:T(8,128)(2,1)S(1)} %copy-done.4), kind=kOutput, calls=%fused_computation.24 | convolution fusion | flops 188743680 | bytes 24543232 | tf_op jit(solution)/shard_map/rhw,rkw->rhk/dot_general | solution.py:69
  238.2 10.2 %fusion.13 = f32[16,32,8,640]{3,2,1,0:T(8,128)} fusion(f32[16,32,8,640]{3,2,1,0:T(8,128)} %fusion.14, bf16[32,640,576]{1,2,0:T(8,128)(2,1)} %constant_dynamic-update-slice_fusion, bf16[32,8,576]{2,1,0:T(8,128)(2,1)S(1)} %copy-done.6), kind=kOutput, calls=%fused_computation.22 | convolution fusion | flops 188743680 | bytes 24543232 | tf_op jit(solution)/shard_map/rhw,rkw->rhk/dot_general | solution.py:69
  248.4 10.3 %fusion.12 = f32[16,32,8,640]{3,2,1,0:T(8,128)} fusion(f32[16,32,8,640]{3,2,1,0:T(8,128)} %fusion.13, bf16[32,640,576]{1,2,0:T(8,128)(2,1)} %constant_dynamic-update-slice_fusion, bf16[32,8,576]{2,1,0:T(8,128)(2,1)} %collective-permute-done.13), kind=kOutput, calls=%fused_computation.20 | convolution fusion | flops 188743680 | bytes 24576000 | tf_op jit(solution)/shard_map/rhw,rkw->rhk/dot_general | solution.py:69
  258.7 10.3 %fusion.11 = f32[16,32,8,640]{3,2,1,0:T(8,128)} fusion(f32[16,32,8,640]{3,2,1,0:T(8,128)} %fusion.12, bf16[32,640,576]{1,2,0:T(8,128)(2,1)} %constant_dynamic-update-slice_fusion, bf16[32,8,576]{2,1,0:T(8,128)(2,1)} %collective-permute-done.14), kind=kOutput, calls=%fused_computation.18 | convolution fusion | flops 188743680 | bytes 24576000 | tf_op jit(solution)/shard_map/rhw,rkw->rhk/dot_general | solution.py:69
  268.9 9.2 %gather_fusion.2 = f32[16,32,8,640]{3,2,1,0:T(8,128)} fusion(f32[16,32,8,640]{3,2,1,0:T(8,128)} %fusion.11, s32[1024]{0:T(1024)} %pad_clamp_fusion), kind=kCustom, calls=%fused_computation.2 | custom fusion | bytes 20971584 | tf_op jit(solution)/shard_map/gather | solution.py:60
  278.1 5.8 %bitcast_reduce_fusion = f32[32,16,8]{2,0,1:T(8,128)S(1)} fusion(f32[16,32,8,640]{3,2,1,0:T(8,128)} %gather_fusion.2, pred[32,640]{1,0:T(8,128)(4,1)S(1)} %copy-done.7), kind=kLoop, calls=%fused_computation.6 | loop fusion | flops 7860224 | bytes 10522624 | tf_op jit(solution)/shard_map/reduce_max | solution.py:77
  284.0 57.7 %pmax.7 = f32[32,128]{0,1:T(8,128)S(1)} all-reduce(f32[32,128]{0,1:T(8,128)S(1)} %bitcast.157), channel_id=1, replica_groups=mesh['groups'=2,'seq'=16] {'seq'}, use_global_device_ids=true, to_apply=%region_4.5 | all-reduce | flops 4096 | bytes 32768 | tf_op jit(solution)/shard_map/pmax | solution.py:77
  341.8 16.7 %fusion = f32[32,128,512]{2,1,0:T(8,128)} fusion(bf16[32,640,576]{1,2,0:T(8,128)(2,1)} %constant_dynamic-update-slice_fusion, f32[32,128]{1,0:T(8,128)S(1)} %copy.30, pred[32,640]{1,0:T(8,128)(4,1)S(1)} %copy-done.7, f32[16,32,8,640]{3,2,1,0:T(8,128)} %gather_fusion.2), kind=kOutput, calls=%fused_computation.3 | convolution fusion | flops 2694840320 | bytes 39882752 | tf_op jit(solution)/shard_map/rhk,rkl->rhl/dot_general | solution.py:81
  358.5 0.6 dynamic-slice
  360.1 9.8 %fusion.3 = f32[32,16,8]{2,0,1:T(8,128)S(1)} fusion(f32[16,32,8,640]{3,2,1,0:T(8,128)} %gather_fusion.2, f32[32,16,8]{2,0,1:T(8,128)S(1)} %copy.32, pred[32,640]{1,0:T(8,128)(4,1)S(1)} %copy-done.7), kind=kLoop, calls=%fused_computation.8 | loop fusion | flops 10481664 | bytes 10539008 | tf_op jit(solution)/shard_map/reduce_sum | solution.py:79
  370.0 60.5 %all-reduce.1 = f32[32,128]{0,1:T(8,128)S(1)} all-reduce(f32[32,128]{0,1:T(8,128)S(1)} %bitcast.158), channel_id=3, replica_groups=mesh['groups'=2,'seq'=16] {'seq'}, use_global_device_ids=true, to_apply=%region_7.8.clone | all-reduce | flops 4096 | bytes 32768
  430.6 29.9 %reduce-scatter.2.cloned.1.call-done = f32[32,8,512]{2,1,0:T(8,128)} async-done(((f32[32,128,512]{2,1,0:T(8,128)}), f32[32,8,512]{2,1,0:T(8,128)}) %reduce-scatter.2.cloned.1.call-update) | async-done | bytes 524304 | tf_op jit(solution)/shard_map/reduce_scatter | solution.py:86
  460.5 1.9 divide_convert_fusion
  (53 shorter events, 0.7 us)
Async XLA Ops:
  6.5 39.8 %copy-start = (bf16[32,64,576]{2,1,0:T(8,128)(2,1)S(1)}, bf16[32,64,576]{2,1,0:T(8,128)(2,1)}, u32[]{:S(2)}) copy-start(bf16[32,64,576]{2,1,0:T(8,128)(2,1)} %param.7) | copy-start | bytes 7077892
  6.5 454.0 %reduce-scatter.2.cloned.1.call-start = ((), (), s32[]{:S(2)}) async-start(), calls=%async_computation.1 | async-start | bytes 8912896 | tf_op jit(solution)/shard_map/reduce_scatter | solution.py:86
  6.5 10.4 %collective-permute-start = (bf16[32,8,576]{2,1,0:T(8,128)(2,1)}, bf16[32,8,576]{2,1,0:T(8,128)(2,1)S(1)}, u32[]{:S(2)}, u32[]{:S(2)}) collective-permute-start(bf16[32,8,576]{2,1,0:T(8,128)(2,1)} %param.6), channel_id=1, source_target_pairs={{0,1},{1,2},{2,3},{3,4},{4,5},{5,6},{6,7},{7,8},{8,9},{9,10},{10,1... | collective-permute-start | bytes 884744 | tf_op jit(solution)/shard_map/ppermute | solution.py:48
  17.0 9.4 %collective-permute-start.1 = (bf16[32,8,576]{2,1,0:T(8,128)(2,1)S(1)}, bf16[32,8,576]{2,1,0:T(8,128)(2,1)}, u32[]{:S(2)}, u32[]{:S(2)}) collective-permute-start(bf16[32,8,576]{2,1,0:T(8,128)(2,1)S(1)} %collective-permute-done), channel_id=1, source_target_pairs={{0,1},{1,2},{2,3},{3,4},{4,5},{5,6},{6,7},{7,8},{8,9},{9,10},{10,1... | collective-permute-start | bytes 884744 | tf_op jit(solution)/shard_map/ppermute | solution.py:48
  17.0 10.3 %collective-permute-start.8 = (bf16[32,8,576]{2,1,0:T(8,128)(2,1)}, bf16[32,8,576]{2,1,0:T(8,128)(2,1)S(1)}, u32[]{:S(2)}, u32[]{:S(2)}) collective-permute-start(bf16[32,8,576]{2,1,0:T(8,128)(2,1)} %param.6), channel_id=1, source_target_pairs={{0,15},{1,0},{2,1},{3,2},{4,3},{5,4},{6,5},{7,6},{8,7},{9,8},{10,9... | collective-permute-start | bytes 884744 | tf_op jit(solution)/shard_map/ppermute | solution.py:50
  26.4 9.6 %collective-permute-start.2 = (bf16[32,8,576]{2,1,0:T(8,128)(2,1)}, bf16[32,8,576]{2,1,0:T(8,128)(2,1)}, u32[]{:S(2)}, u32[]{:S(2)}) collective-permute-start(bf16[32,8,576]{2,1,0:T(8,128)(2,1)} %collective-permute-done.1), channel_id=1, source_target_pairs={{0,1},{1,2},{2,3},{3,4},{4,5},{5,6},{6,7},{7,8},{8,9},{9,10},{10,1... | collective-permute-start | bytes 884744 | tf_op jit(solution)/shard_map/ppermute | solution.py:48
  27.3 10.3 %collective-permute-start.9 = (bf16[32,8,576]{2,1,0:T(8,128)(2,1)S(1)}, bf16[32,8,576]{2,1,0:T(8,128)(2,1)}, u32[]{:S(2)}, u32[]{:S(2)}) collective-permute-start(bf16[32,8,576]{2,1,0:T(8,128)(2,1)S(1)} %collective-permute-done.8), channel_id=1, source_target_pairs={{0,15},{1,0},{2,1},{3,2},{4,3},{5,4},{6,5},{7,6},{8,7},{9,8},{10,9... | collective-permute-start | bytes 884744 | tf_op jit(solution)/shard_map/ppermute | solution.py:50
  36.0 9.6 %collective-permute-start.3 = (bf16[32,8,576]{2,1,0:T(8,128)(2,1)}, bf16[32,8,576]{2,1,0:T(8,128)(2,1)}, u32[]{:S(2)}, u32[]{:S(2)}) collective-permute-start(bf16[32,8,576]{2,1,0:T(8,128)(2,1)} %collective-permute-done.2), channel_id=1, source_target_pairs={{0,1},{1,2},{2,3},{3,4},{4,5},{5,6},{6,7},{7,8},{8,9},{9,10},{10,1... | collective-permute-start | bytes 884744 | tf_op jit(solution)/shard_map/ppermute | solution.py:48
  37.6 21.9 %collective-permute-start.10 = (bf16[32,8,576]{2,1,0:T(8,128)(2,1)}, bf16[32,8,576]{2,1,0:T(8,128)(2,1)}, u32[]{:S(2)}, u32[]{:S(2)}) collective-permute-start(bf16[32,8,576]{2,1,0:T(8,128)(2,1)} %collective-permute-done.9), channel_id=1, source_target_pairs={{0,15},{1,0},{2,1},{3,2},{4,3},{5,4},{6,5},{7,6},{8,7},{9,8},{10,9... | collective-permute-start | bytes 884744 | tf_op jit(solution)/shard_map/ppermute | solution.py:50
  45.6 18.4 %collective-permute-start.4 = (bf16[32,8,576]{2,1,0:T(8,128)(2,1)}, bf16[32,8,576]{2,1,0:T(8,128)(2,1)}, u32[]{:S(2)}, u32[]{:S(2)}) collective-permute-start(bf16[32,8,576]{2,1,0:T(8,128)(2,1)} %collective-permute-done.3), channel_id=1, source_target_pairs={{0,1},{1,2},{2,3},{3,4},{4,5},{5,6},{6,7},{7,8},{8,9},{9,10},{10,1... | collective-permute-start | bytes 884744 | tf_op jit(solution)/shard_map/ppermute | solution.py:48
  59.6 25.8 %copy-start.8 = (s32[32]{0:T(128)S(1)}, s32[32]{0:T(128)}, u32[]{:S(2)}) copy-start(s32[32]{0:T(128)} %param.11) | copy-start | bytes 388
  59.6 21.3 %collective-permute-start.11 = (bf16[32,8,576]{2,1,0:T(8,128)(2,1)}, bf16[32,8,576]{2,1,0:T(8,128)(2,1)S(1)}, u32[]{:S(2)}, u32[]{:S(2)}) collective-permute-start(bf16[32,8,576]{2,1,0:T(8,128)(2,1)} %collective-permute-done.10), channel_id=1, source_target_pairs={{0,15},{1,0},{2,1},{3,2},{4,3},{5,4},{6,5},{7,6},{8,7},{9,8},{10,9... | collective-permute-start | bytes 884744 | tf_op jit(solution)/shard_map/ppermute | solution.py:50
  64.0 21.4 %collective-permute-start.5 = (bf16[32,8,576]{2,1,0:T(8,128)(2,1)}, bf16[32,8,576]{2,1,0:T(8,128)(2,1)S(1)}, u32[]{:S(2)}, u32[]{:S(2)}) collective-permute-start(bf16[32,8,576]{2,1,0:T(8,128)(2,1)} %collective-permute-done.4), channel_id=1, source_target_pairs={{0,1},{1,2},{2,3},{3,4},{4,5},{5,6},{6,7},{7,8},{8,9},{9,10},{10,1... | collective-permute-start | bytes 884744 | tf_op jit(solution)/shard_map/ppermute | solution.py:48
  80.9 34.1 %copy-start.3 = (bf16[32,8,576]{2,1,0:T(8,128)(2,1)}, bf16[32,8,576]{2,1,0:T(8,128)(2,1)S(1)}, u32[]{:S(2)}) copy-start(bf16[32,8,576]{2,1,0:T(8,128)(2,1)S(1)} %collective-permute-done.11) | copy-start | bytes 884740
  80.9 9.1 %collective-permute-start.12 = (bf16[32,8,576]{2,1,0:T(8,128)(2,1)S(1)}, bf16[32,8,576]{2,1,0:T(8,128)(2,1)S(1)}, u32[]{:S(2)}, u32[]{:S(2)}) collective-permute-start(bf16[32,8,576]{2,1,0:T(8,128)(2,1)S(1)} %collective-permute-done.11), channel_id=1, source_target_pairs={{0,15},{1,0},{2,1},{3,2},{4,3},{5,4},{6,5},{7,6},{8,7},{9,8},{10,9... | collective-permute-start | bytes 884744 | tf_op jit(solution)/shard_map/ppermute | solution.py:50
  85.4 9.3 %collective-permute-start.6 = (bf16[32,8,576]{2,1,0:T(8,128)(2,1)S(1)}, bf16[32,8,576]{2,1,0:T(8,128)(2,1)S(1)}, u32[]{:S(2)}, u32[]{:S(2)}) collective-permute-start(bf16[32,8,576]{2,1,0:T(8,128)(2,1)S(1)} %collective-permute-done.5), channel_id=1, source_target_pairs={{0,1},{1,2},{2,3},{3,4},{4,5},{5,6},{6,7},{7,8},{8,9},{9,10},{10,1... | collective-permute-start | bytes 884744 | tf_op jit(solution)/shard_map/ppermute | solution.py:48
  90.0 25.0 %copy-start.5 = (bf16[32,8,576]{2,1,0:T(8,128)(2,1)}, bf16[32,8,576]{2,1,0:T(8,128)(2,1)S(1)}, u32[]{:S(2)}) copy-start(bf16[32,8,576]{2,1,0:T(8,128)(2,1)S(1)} %collective-permute-done.12) | copy-start | bytes 884740
  90.0 10.3 %collective-permute-start.13 = (bf16[32,8,576]{2,1,0:T(8,128)(2,1)S(1)}, bf16[32,8,576]{2,1,0:T(8,128)(2,1)}, u32[]{:S(2)}, u32[]{:S(2)}) collective-permute-start(bf16[32,8,576]{2,1,0:T(8,128)(2,1)S(1)} %collective-permute-done.12), channel_id=1, source_target_pairs={{0,15},{1,0},{2,1},{3,2},{4,3},{5,4},{6,5},{7,6},{8,7},{9,8},{10,9... | collective-permute-start | bytes 884744 | tf_op jit(solution)/shard_map/ppermute | solution.py:50
  94.7 10.0 %collective-permute-start.7 = (bf16[32,8,576]{2,1,0:T(8,128)(2,1)S(1)}, bf16[32,8,576]{2,1,0:T(8,128)(2,1)S(1)}, u32[]{:S(2)}, u32[]{:S(2)}) collective-permute-start(bf16[32,8,576]{2,1,0:T(8,128)(2,1)S(1)} %collective-permute-done.6), channel_id=1, source_target_pairs={{0,1},{1,2},{2,3},{3,4},{4,5},{5,6},{6,7},{7,8},{8,9},{9,10},{10,1... | collective-permute-start | bytes 884744 | tf_op jit(solution)/shard_map/ppermute | solution.py:48
  100.3 158.4 %collective-permute-start.14 = (bf16[32,8,576]{2,1,0:T(8,128)(2,1)}, bf16[32,8,576]{2,1,0:T(8,128)(2,1)}, u32[]{:S(2)}, u32[]{:S(2)}) collective-permute-start(bf16[32,8,576]{2,1,0:T(8,128)(2,1)} %collective-permute-done.13), channel_id=1, source_target_pairs={{0,15},{1,0},{2,1},{3,2},{4,3},{5,4},{6,5},{7,6},{8,7},{9,8},{10,9... | collective-permute-start | bytes 884744 | tf_op jit(solution)/shard_map/ppermute | solution.py:50
  176.6 10.3 %copy-start.2 = (bf16[32,8,576]{2,1,0:T(8,128)(2,1)S(1)}, bf16[32,8,576]{2,1,0:T(8,128)(2,1)}, u32[]{:S(2)}) copy-start(bf16[32,8,576]{2,1,0:T(8,128)(2,1)} %param.6) | copy-start | bytes 884740
  217.5 10.3 %copy-start.4 = (bf16[32,8,576]{2,1,0:T(8,128)(2,1)S(1)}, bf16[32,8,576]{2,1,0:T(8,128)(2,1)}, u32[]{:S(2)}) copy-start(bf16[32,8,576]{2,1,0:T(8,128)(2,1)} %copy-done.3) | copy-start | bytes 884740
  227.9 10.3 %copy-start.6 = (bf16[32,8,576]{2,1,0:T(8,128)(2,1)S(1)}, bf16[32,8,576]{2,1,0:T(8,128)(2,1)}, u32[]{:S(2)}) copy-start(bf16[32,8,576]{2,1,0:T(8,128)(2,1)} %copy-done.5) | copy-start | bytes 884740
  268.9 9.2 %copy-start.7 = (pred[32,640]{1,0:T(8,128)(4,1)S(1)}, pred[32,640]{1,0:T(8,128)(4,1)}, u32[]{:S(2)}) copy-start(pred[32,640]{1,0:T(8,128)(4,1)} %concatenate.6) | copy-start | bytes 61444
  341.8 16.8 %copy-start.9 = (u32[32]{0:T(128)S(1)}, u32[32]{0:T(128)}, u32[]{:S(2)}) copy-start(u32[32]{0:T(128)} %constant.48) | copy-start | bytes 388
  358.5 103.9 %copy-start.1 = (bf16[32,64,576]{2,1,0:T(8,128)(2,1)S(1)}, bf16[32,64,576]{2,1,0:T(8,128)(2,1)}, u32[]{:S(2)}) copy-start(bf16[32,64,576]{2,1,0:T(8,128)(2,1)} %param.7) | copy-start | bytes 7077892
Sparse Core Ops, SparseCore 0:
  358.6 101.8 reduce-scatter.1
